TPU v7x, 32 devices: a whole 2x2x4 slice. The times are simulated.
32 devices in a mesh: grp: 2 (over y), band: 4 (over x, core), ga: 4 (over z).
Axes of the slice: x: 2, y: 2, z: 4, core: 2. Of those that a mesh axis runs over, the one named last changes fastest.
Arguments:
- orbitals: bfloat16 [64, 8192], P(('grp', 'band'), 'ga'), parts along dimension 0, may hold values from -0.0625 to 0.0625
- energies: float32 [64], P(('grp', 'band')), parts along dimension 0, may hold values from -1.5 to -0.2
- projectors: bfloat16 [1024, 8192], P('grp', 'ga'), parts along dimension 0, may hold values from -0.125 to 0.125
- miller_index: int32 [3, 8192], P(None, 'ga'), may hold values from -12 to 12
- recip_scale: float32 [6], P('grp'), parts along dimension 0, may hold values from 0.06 to 0.14
- species: int32 [128], replicated, may hold values from 0 to 2
- proj_atom: int32 [512], replicated, may hold values from 0 to 127, as said below
- coupling: float32 [3, 4], replicated, may hold values from 0.5 to 3
Outputs:
- response: bfloat16 [3, 64, 8192], P(None, ('grp', 'band'), 'ga'), parts along dimension 1
- dielectric: float32 [6, 3], P('grp'), parts along dimension 0
- born: float32 [9, 256], P(None, 'grp'), parts along dimension 1
There are 2 independent parts, one for each index of `grp`. A program takes and returns all parts, laid end to end along the dimension named above; an argument that names none is the same for every part. Nothing has to cross between parts.
Inputs may be any that keep to these rules, and one draw needn't show every extreme that they name: `proj_atom`: every atom owns exactly 4 projectors.
All inputs are finite; a program needn't handle non-finite values.
Results may differ from a plain program's by a relative error of at most 0.015.
Values may be sent and summed in bfloat16 or wider, within the bound.
A program may use at most 64 MiB of HBM per device.

v0:
```python
import jax
import jax.numpy as jnp
from jax import lax
from jax.sharding import PartitionSpec as P

ITERS = 2


born_scale = 40.0


def tables(miller_index, recip_scale, species, proj_atom, coupling):
    natoms = species.shape[0]
    nspecies = coupling.shape[0]
    nchannels = coupling.shape[1]
    wavevec = miller_index.astype(jnp.float32) * recip_scale[:, None]
    kinetic = 0.5 * jnp.sum(wavevec * wavevec, axis=0)
    atom_onehot = (proj_atom[:, None] == jnp.arange(natoms, dtype=jnp.int32)[None, :]).astype(
        jnp.float32
    )
    spec_proj = jnp.dot(atom_onehot, species.astype(jnp.float32), precision=lax.Precision.HIGHEST)
    spec_onehot = (spec_proj[:, None] == jnp.arange(nspecies, dtype=jnp.float32)[None, :]).astype(
        jnp.float32
    )
    channel = jnp.arange(proj_atom.shape[0], dtype=jnp.int32) % nchannels
    chan_onehot = (channel[:, None] == jnp.arange(nchannels, dtype=jnp.int32)[None, :]).astype(
        jnp.float32
    )
    strength = jnp.sum(
        jnp.dot(spec_onehot, coupling, precision=lax.Precision.HIGHEST) * chan_onehot, axis=1
    )
    return (wavevec, kinetic, atom_onehot, strength)


def per_device(
    orbitals, energies, projectors, miller_index, recip_scale, species, proj_atom, coupling
):
    bands = orbitals.shape[0]
    width = orbitals.shape[1]
    nproj = projectors.shape[0]
    total_bands = bands * lax.axis_size("band")
    wavevec, kinetic, atom_onehot, strength = tables(
        miller_index, recip_scale, species, proj_atom, coupling
    )
    precond = 1.0 / (1.0 + kinetic)

    def conduct(values):
        flat = values.reshape(3 * bands, width)
        block = jnp.dot(
            lax.all_gather(orbitals, "band", axis=0, tiled=True),
            flat.T,
            preferred_element_type=jnp.float32,
        )
        margin = lax.psum(block, "ga").astype(jnp.bfloat16)
        removed = jnp.dot(
            margin.T,
            lax.all_gather(orbitals, "band", axis=0, tiled=True),
            preferred_element_type=jnp.float32,
        )
        return (flat.astype(jnp.float32) - removed).reshape(3, bands, width)

    orb_float = orbitals.astype(jnp.float32)
    stacked = jnp.concatenate([orb_float[None], wavevec[:, None, :] * orb_float[None]], 0).astype(
        jnp.bfloat16
    )
    proj_local = jnp.dot(
        stacked.reshape(4 * bands, width), projectors.T, preferred_element_type=jnp.float32
    )
    proj = lax.psum(proj_local, "ga").reshape(4, bands, nproj)
    weighted = (strength * proj).astype(jnp.bfloat16)
    returned = jnp.dot(
        weighted.reshape(4 * bands, nproj), projectors, preferred_element_type=jnp.float32
    ).reshape(4, bands, width)
    commutator = (wavevec[:, None, :] * (orb_float + returned[0])[None] + returned[1:]).astype(
        jnp.bfloat16
    )
    source = -conduct(commutator)
    response = jnp.zeros_like(source)
    residual = source
    resp_proj = jnp.zeros((3, bands, nproj), jnp.float32)
    diag_shift = kinetic[None, None, :] - energies[None, :, None]
    for step in range(ITERS):
        search = conduct((precond * residual).astype(jnp.bfloat16))
        search_low = search.astype(jnp.bfloat16)
        dir_local = jnp.dot(
            search_low.reshape(3 * bands, width), projectors.T, preferred_element_type=jnp.float32
        )
        num_local = jnp.sum(residual * search, axis=2)
        diag_local = jnp.sum(diag_shift * search * search, axis=2)
        dir_proj, numerator, diag_part = lax.psum((dir_local, num_local, diag_local), "ga")
        dir_proj = dir_proj.reshape(3, bands, nproj)
        dir_weight = (strength * dir_proj).astype(jnp.bfloat16)
        image = diag_shift * search + jnp.dot(
            dir_weight.reshape(3 * bands, nproj), projectors, preferred_element_type=jnp.float32
        ).reshape(3, bands, width)
        curvature = diag_part + jnp.sum(dir_weight.astype(jnp.float32) * dir_proj, axis=2)
        step_size = numerator / curvature
        response = response + step_size[:, :, None] * search
        residual = residual - step_size[:, :, None] * image
        resp_proj = resp_proj + step_size[:, :, None] * dir_proj
    diel_local = jnp.einsum("anx,bnx->ab", response, source, precision=lax.Precision.HIGHEST)
    dielectric = jnp.eye(3, dtype=jnp.float32) + 4.0 / total_bands * lax.psum(
        diel_local, ("band", "ga")
    )
    pair = jnp.einsum("anp,bnp->abp", resp_proj, proj[1:], precision=lax.Precision.HIGHEST)
    born_local = jnp.dot(
        (pair * strength).reshape(9, nproj), atom_onehot, precision=lax.Precision.HIGHEST
    )
    born = born_scale * lax.psum(born_local, "band")
    return (response.astype(jnp.bfloat16), dielectric, born)


def solution(mesh):
    placed = (
        P(("grp", "band"), "ga"),
        P(("grp", "band")),
        P("grp", "ga"),
        P(None, "ga"),
        P("grp"),
        P(),
        P(),
        P(),
    )
    return jax.shard_map(
        per_device,
        mesh=mesh,
        in_specs=placed,
        out_specs=(P(None, ("grp", "band"), "ga"), P("grp", None), P(None, "grp")),
        check_vma=False,
    )
```

profile of v0, /device:TPU:0, one launch (start us, length us, event | category | flops | bytes accessed | tf_op | source)
XLA Modules:
  0.0 192.2 jit_solution(5939086287881664296)
XLA Ops:
  7.2 0.0 all-reduce.4.cloned.1.call-start
  7.3 0.9 convert_element_type.82
  8.2 0.9 multiply_reduce_fusion.3
  9.1 2.1 %fusion.18 = f32[32,512]{1,0:T(8,128)} fusion(bf16[512,2048]{1,0:T(8,128)(2,1)S(1)} %copy-done, bf16[3,8,2048]{2,1,0:T(8,128)(2,1)S(1)} %multiply_convert_fusion.2, bf16[1,8,2048]{2,1,0:T(8,128)(2,1)} %bitcast.93), kind=kOutput, calls=%fused_computation.43 | convolution fusion | flops 67174400 | bytes 2293760 | tf_op jit(solution)/shard_map/dot_general | solution.py:66
  11.2 0.0 all-reduce.4.cloned.1.call-update
  11.3 0.3 fusion.11
  11.6 0.1 broadcast_subtract_fusion
  11.7 0.4 fusion.5
  12.0 6.5 %all_gather.2 = bf16[32,2048]{1,0:T(8,128)(2,1)S(1)} all-gather(bf16[8,2048]{1,0:T(8,128)(2,1)S(1)} %copy-done.1), channel_id=1, replica_groups=mesh['grp'=2,'band'=4,'ga'=4] {'band'}, dimensions={0}, use_global_device_ids=true | all-gather | bytes 163840 | tf_op jit(solution)/shard_map/all_gather | solution.py:50
  18.5 29.9 %all-reduce.4.cloned.1.call-done = f32[32,512]{1,0:T(8,128)} async-done(((f32[32,512]{1,0:T(8,128)}), f32[32,512]{1,0:T(8,128)}) %all-reduce.4.cloned.1.call-update) | async-done | bytes 65552 | tf_op jit(solution)/shard_map/psum | solution.py:69
  48.4 1.3 fusion.32
  49.8 0.2 convolution_bitcast_fusion.2
  49.9 17.5 %psum.85 = bf16[32,24]{0,1:T(8,128)(2,1)S(1)} all-reduce(f32[32,24]{0,1:T(8,128)S(1)} %convolution_bitcast_fusion.2), channel_id=1, replica_groups=mesh['grp'=2,'band'=4,'ga'=4] {'ga'}, use_global_device_ids=true, to_apply=%region_2.3 | all-reduce | flops 768 | bytes 4608 | tf_op jit(solution)/shard_map/psum | solution.py:54
  67.4 0.2 fusion
  67.6 0.2 convolution_bitcast_fusion.1
  67.7 15.6 %psum.86 = bf16[32,24]{0,1:T(8,128)(2,1)S(1)} all-reduce(f32[32,24]{0,1:T(8,128)S(1)} %convolution_bitcast_fusion.1), channel_id=1, replica_groups=mesh['grp'=2,'band'=4,'ga'=4] {'ga'}, use_global_device_ids=true, to_apply=%region_4.5 | all-reduce | flops 768 | bytes 4608 | tf_op jit(solution)/shard_map/psum | solution.py:54
  83.3 0.3 fusion.13
  83.6 0.1 reduce_sum.87
  83.7 0.1 reduce_sum.85
  83.8 0.7 fusion.27
  84.5 17.3 %all-reduce.1 = (f32[3,8]{1,0:T(4,128)S(1)}, f32[3,8]{1,0:T(4,128)S(1)}, f32[24,512]{1,0:T(8,128)S(1)}) all-reduce(f32[3,8]{1,0:T(4,128)S(1)} %reduce_sum.85, f32[3,8]{1,0:T(4,128)S(1)} %reduce_sum.87, f32[24,512]{1,0:T(8,128)S(1)} %fusion.27), channel_id=1, replica_groups=mesh['grp'=2,'band'=4,'ga'=4] {'ga'}, use_global_device_ids=true, to_apply=%region_6.7 | all-reduce | flops 12336 | bytes 98688 | tf_op jit(solution)/shard_map/psum | solution.py:90
  101.7 0.1 multiply_reduce_fusion.2
  101.8 0.1 reduce_sum.89
  101.9 0.1 mul.254
  102.0 0.4 fusion.2
  102.4 0.2 convolution_bitcast_fusion
  102.6 16.5 %psum.90 = bf16[32,24]{0,1:T(8,128)(2,1)S(1)} all-reduce(f32[32,24]{0,1:T(8,128)S(1)} %convolution_bitcast_fusion), channel_id=1, replica_groups=mesh['grp'=2,'band'=4,'ga'=4] {'ga'}, use_global_device_ids=true, to_apply=%region_11.12 | all-reduce | flops 768 | bytes 4608 | tf_op jit(solution)/shard_map/psum | solution.py:54
  119.1 0.2 fusion.15
  119.3 0.1 fusion.12
  119.5 0.7 fusion.25
  120.1 0.1 reduce_sum.92
  120.2 16.3 %all-reduce = (f32[3,8]{1,0:T(4,128)S(1)}, f32[3,8]{1,0:T(4,128)S(1)}, f32[24,512]{1,0:T(8,128)S(1)}) all-reduce(f32[3,8]{1,0:T(4,128)S(1)} %get-tuple-element.16, f32[3,8]{1,0:T(4,128)S(1)} %reduce_sum.92, f32[24,512]{1,0:T(8,128)S(1)} %fusion.25), channel_id=1, replica_groups=mesh['grp'=2,'band'=4,'ga'=4] {'ga'}, use_global_device_ids=true, to_apply=%region_13.14 | all-reduce | flops 12336 | bytes 98688 | tf_op jit(solution)/shard_map/psum | solution.py:90
  136.6 0.1 multiply_reduce_fusion.1
  136.7 0.1 reduce_sum.94
  136.8 0.1 mul.257
  136.8 0.7 fusion.17
  137.6 0.1 add_bitcast_fusion
  137.7 1.4 convolution_bitcast_fusion.3
  139.0 0.1 fusion.29
  139.1 29.7 %psum.94 = f32[3,3]{1,0:T(4,128)S(1)} all-reduce(f32[3,3]{1,0:T(4,128)S(1)} %convolution_bitcast_fusion.3), channel_id=1, replica_groups=mesh['grp'=2,'band'=4,'ga'=4] {'band','ga'}, use_global_device_ids=true, to_apply=%region_18.19 | all-reduce | flops 9 | bytes 72 | tf_op jit(solution)/shard_map/psum | solution.py:102
  168.9 0.6 multiply_add_fusion
  169.5 0.4 copy.25
  169.9 1.3 copy.24
  171.2 5.9 %fusion.4 = f32[3,3,512]{0,1,2:T(4,128)} fusion(f32[3,8,512]{1,0,2:T(4,128)} %copy.24, f32[3,8,512]{1,0,2:T(4,128)S(1)} %copy.25, f32[512]{0:T(512)S(1)} %fusion.5), kind=kOutput, calls=%fused_computation.9 | convolution fusion | flops 446976 | bytes 118784 | tf_op jit(solution)/shard_map/anp,bnp->abp/dot_general | solution.py:105
  177.1 1.6 copy.26
  178.7 0.3 fusion.10
  179.0 5.8 %psum.95 = f32[9,128]{1,0:T(8,128)S(1)} all-reduce(f32[9,128]{1,0:T(8,128)S(1)} %fusion.10), channel_id=1, replica_groups=mesh['grp'=2,'band'=4,'ga'=4] {'band'}, use_global_device_ids=true, to_apply=%region_19.20 | all-reduce | flops 1152 | bytes 9216 | tf_op jit(solution)/shard_map/psum | solution.py:109
  184.8 0.6 broadcast_multiply_fusion
  (22 shorter events, 0.1 us)
Async XLA Ops:
  7.2 1.9 copy-start
  7.2 4.8 %copy-start.1 = (bf16[8,2048]{1,0:T(8,128)(2,1)S(1)}, bf16[8,2048]{1,0:T(8,128)(2,1)}, u32[]{:S(2)}) copy-start(bf16[8,2048]{1,0:T(8,128)(2,1)} %param.8) | copy-start | bytes 98308
  7.2 4.1 %copy-start.5 = (s32[512]{0:T(512)S(1)}, s32[512]{0:T(512)}, u32[]{:S(2)}) copy-start(s32[512]{0:T(512)} %param.14) | copy-start | bytes 6148
  7.2 4.1 %copy-start.6 = (s32[128]{0:T(128)S(1)}, s32[128]{0:T(128)}, u32[]{:S(2)}) copy-start(s32[128]{0:T(128)} %param.13) | copy-start | bytes 1540
  7.2 4.4 %copy-start.3 = (f32[8]{0:T(128)S(1)}, f32[8]{0:T(128)}, u32[]{:S(2)}) copy-start(f32[8]{0:T(128)} %param.9) | copy-start | bytes 100
  7.2 4.4 %copy-start.4 = (f32[3,4]{1,0:T(4,128)S(1)}, f32[3,4]{1,0:T(4,128)}, u32[]{:S(2)}) copy-start(f32[3,4]{1,0:T(4,128)} %param.15) | copy-start | bytes 148
  7.2 41.2 %all-reduce.4.cloned.1.call-start = ((), (), s32[]{:S(2)}) async-start(), calls=%async_computation | async-start | bytes 131072 | tf_op jit(solution)/shard_map/psum | solution.py:69
  119.5 50.4 %copy-start.2 = (f32[32,512]{1,0:T(8,128)S(1)}, f32[32,512]{1,0:T(8,128)}, u32[]{:S(2)}) copy-start(f32[32,512]{1,0:T(8,128)} %all-reduce.4.cloned.1.call-done) | copy-start | bytes 196612
Sparse Core Ops, SparseCore 0:
  11.3 37.0 all-reduce.3
where the time goes:
time: 193 us; the launch traced here: 192 us
  blocking collectives  125 us (65%)
  waiting for transfers between devices  29.9 us (15%)
  matrix products  14.5 us (8%)
  between operations  14.2 us (7%)
  other arithmetic  4.39 us (2%)
  local copies, waits for them, and re-layouts  3.93 us (2%)
    psum x3, blocking collectives, conduct(): margin = lax.psum(block, 'ga').astype(jnp.bfloat16)  49.6 us
    psum x2, blocking collectives, per_device(): lax.psum((dir_local, num_local, diag_local), 'ga')  33.6 us
    psum x1, waiting for transfers between devices, per_device(): proj = lax.psum(proj_local, 'ga').reshape(4, bands, nproj)  29.9 us
    psum x1, blocking collectives, per_device(): lax.psum(diel_local, ('band', 'ga'))  29.7 us
    all_gather x1, blocking collectives, conduct(): lax.all_gather(orbitals, 'band', axis=0, tiled=True)  6.51 us
    dot_general x1, matrix products, per_device(): jnp.einsum('anp,bnp->abp', resp_proj, proj[1:], precision=lax.Precision.H...  5.93 us
    psum x1, blocking collectives, per_device(): born = born_scale * lax.psum(born_local, 'band')  5.77 us
  transfers between devices with their start and end apart: 1, of which 1 were waited for; matrix products, arithmetic and copies ran while one was open for 0% of the time, Pallas kernels for 0%

commit v1 on v0

v1 whole, which is shorter than its diff:
```python
import functools

import jax
import jax.numpy as jnp
from jax import lax
from jax.experimental import pallas as pl
from jax.experimental.pallas import tpu as pltpu
from jax.sharding import PartitionSpec as P

ITERS = 2
BORN_SCALE = 40.0
MESH = pl.DeviceIdType.MESH
F32 = jnp.float32
BF16 = jnp.bfloat16
NT = (((1,), (1,)), ((), ()))
NN = (((1,), (0,)), ((), ()))


def mm(a, b, dims, precision=None):
    return lax.dot_general(a, b, dims, preferred_element_type=F32, precision=precision)


class Exchange:
    def __init__(self, buf, send, recv, axis, n, me, pick=()):
        self.copies = []
        self.arrivals = []
        for off in range(1, n):
            peer = lax.rem(me + off, n)
            src = buf.at[(me,) + pick]
            self.copies.append(
                pltpu.make_async_remote_copy(
                    src_ref=src,
                    dst_ref=src,
                    send_sem=send.at[off],
                    recv_sem=recv.at[me],
                    device_id={axis: peer},
                    device_id_type=MESH,
                )
            )
            other = buf.at[(peer,) + pick]
            self.arrivals.append(
                pltpu.make_async_remote_copy(
                    src_ref=other,
                    dst_ref=other,
                    send_sem=send.at[off],
                    recv_sem=recv.at[peer],
                    device_id={axis: peer},
                    device_id_type=MESH,
                )
            )

    def start(self):
        for copy in self.copies:
            copy.start()
        return self

    def wait(self):
        for arrival in self.arrivals:
            arrival.wait_recv()

    def drain(self):
        for copy in self.copies:
            copy.wait_send()


def total(buf, n):
    acc = buf[0].astype(F32)
    for j in range(1, n):
        acc = acc + buf[j].astype(F32)
    return acc


def kernel(
    nga,
    nband,
    pchunks,
    orb_ref,
    energy_ref,
    proj_hbm,
    miller_ref,
    recip_ref,
    species_ref,
    atom_ref,
    coupling_ref,
    resp_ref,
    diel_ref,
    born_ref,
    pv,
    oall,
    ofull,
    okall,
    r1,
    kk,
    kall,
    kfull,
    gram,
    r2,
    dir3,
    sm3,
    dir4,
    sm4,
    fin,
    pairs,
    psem,
    *sems,
):
    bands, width = orb_ref.shape
    nproj = pv.shape[0]
    tb = bands * nband
    rows = 3 * bands
    ga = lax.axis_index("ga")
    bd = lax.axis_index("band")
    pc = nproj // pchunks

    barrier = pltpu.get_barrier_semaphore()
    for off in range(1, nga):
        pl.semaphore_signal(
            barrier, inc=1, device_id={"ga": lax.rem(ga + off, nga)}, device_id_type=MESH
        )
    for off in range(1, nband):
        pl.semaphore_signal(
            barrier, inc=1, device_id={"band": lax.rem(bd + off, nband)}, device_id_type=MESH
        )
    loads = []
    for k in range(pchunks):
        part = pl.ds(k * pc, pc)
        loads.append(pltpu.make_async_copy(proj_hbm.at[part], pv.at[part], psem.at[k]))
        loads[-1].start()

    it = iter(sems)

    def exchange(buf, axis, pick=()):
        n, me = (nga, ga) if axis == "ga" else (nband, bd)
        return Exchange(buf, next(it), next(it), axis, n, me, pick)

    orb = orb_ref[...].astype(F32)
    wave = [miller_ref[d : d + 1, :].astype(F32) * recip_ref[d] for d in range(3)]
    kinetic = 0.5 * (wave[0] * wave[0] + wave[1] * wave[1] + wave[2] * wave[2])
    precond = 1.0 / (1.0 + kinetic)
    stacked = jnp.concatenate(
        [orb] + [wave[d] * orb for d in range(3)] + [precond * orb], axis=0
    ).astype(BF16)

    band_row = lax.broadcasted_iota(jnp.int32, (bands, 1), 0)
    ecol = jnp.zeros((bands, 1), F32)
    for n in range(bands):
        ecol = jnp.where(band_row == n, energy_ref[n], ecol)
    shift = kinetic - ecol
    shift = jnp.concatenate([shift] * 3, axis=0)

    natoms = species_ref.shape[1]
    atoms = lax.broadcasted_iota(jnp.int32, (natoms, nproj), 0)
    onehot = (atoms == atom_ref[...]).astype(BF16)
    species = species_ref[...].astype(F32)
    spec_rows = jnp.concatenate([species] * 8, axis=0).astype(BF16)
    spec = mm(spec_rows, onehot, NN)[0:1]
    nspec, nchan = coupling_ref.shape
    chan = lax.rem(lax.broadcasted_iota(jnp.int32, (1, nproj), 1), nchan)
    strength = jnp.zeros((1, nproj), F32)
    for s in range(nspec):
        for c in range(nchan):
            strength = jnp.where(
                jnp.logical_and(spec == float(s), chan == c), coupling_ref[s, c], strength
            )

    pl.semaphore_wait(barrier, nga + nband - 2)

    oall[bd] = orb_ref[...]
    x0 = exchange(oall, "band").start()

    x1 = []
    for k in range(pchunks):
        loads[k].wait()
        part = pl.ds(k * pc, pc)
        piece = mm(stacked, pv[part, :], NT)
        r1[ga, :, part] = piece[: 4 * bands].astype(BF16)
        kk[ga, :, part] = piece[4 * bands :].astype(BF16)
        x1.append(exchange(r1, "ga", (slice(None), part)).start())
    xk = exchange(kk, "ga").start()

    x0.wait()
    for j in range(nband):
        ofull[j * bands : (j + 1) * bands, :] = oall[j].astype(F32)
    occupied = ofull[...].astype(BF16)
    okall[:tb, :] = occupied
    okall[tb:, :] = (precond * ofull[...]).astype(BF16)
    gram[ga] = mm(occupied, okall[tb:, :], NT)
    xg = exchange(gram, "ga").start()

    for x in x1:
        x.wait()
    proj = total(r1, nga)
    weighted = (strength * proj).astype(BF16)
    returned = mm(weighted, pv[...], NN)
    inner = orb + returned[:bands]
    comm = jnp.concatenate(
        [wave[d] * inner + returned[(1 + d) * bands : (2 + d) * bands] for d in range(3)], axis=0
    ).astype(BF16)
    r2[ga] = mm(comm, okall[...], NT)
    x2 = exchange(r2, "ga").start()

    xk.wait()
    kall[bd] = total(kk, nga).astype(BF16)
    xa = exchange(kall, "band").start()

    xg.wait()
    gram_all = total(gram, nga)
    x2.wait()
    both = total(r2, nga)
    margin = both[:, :tb].astype(BF16)
    margin_next = mm(margin.astype(F32), gram_all, NN, lax.Precision.HIGHEST) - both[:, tb:]
    removed = mm(
        jnp.concatenate([margin.astype(F32), margin_next], axis=0).astype(BF16),
        okall[:tb, :],
        NN,
    )
    source = removed[:rows] - comm.astype(F32)
    search = (precond * source).astype(BF16).astype(F32) - removed[rows:]

    def send_direction(found, buf):
        low = found.astype(BF16)
        out = []
        for k in range(pchunks):
            part = pl.ds(k * pc, pc)
            buf[ga, :, part] = mm(low, pv[part, :], NT).astype(BF16)
            out.append(exchange(buf, "ga", (slice(None), part)).start())
        return out

    def overlaps(found):
        return [
            jnp.sum(
                found * jnp.concatenate([source[b * bands : (b + 1) * bands]] * 3, axis=0),
                axis=1,
                keepdims=True,
            )
            for b in range(3)
        ]

    def step_of(buf, small, col):
        dp = total(buf, nga)
        dw = (strength * dp).astype(BF16)
        curvature = small[:, col + 1 : col + 2] + jnp.sum(
            dw.astype(F32) * dp, axis=1, keepdims=True
        )
        return dp, dw, small[:, col : col + 1] / curvature

    x3 = send_direction(search, dir3)
    shifted = shift * search
    sm3[ga, :, :tb] = mm((precond * shifted).astype(BF16), okall[:tb, :], NT)
    sm3[ga, :, tb : tb + 1] = jnp.sum(source * search, axis=1, keepdims=True)
    sm3[ga, :, tb + 1 : tb + 2] = jnp.sum(shifted * search, axis=1, keepdims=True)
    x3.append(exchange(sm3, "ga").start())

    for b, col in enumerate(overlaps(search)):
        sm4[ga, :, 2 + b : 3 + b] = col
    xa.wait()
    for j in range(nband):
        kfull[j * bands : (j + 1) * bands, :] = kall[j].astype(F32)
    kp = kfull[...].astype(BF16)

    for x in x3:
        x.wait()
    small3 = total(sm3, nga)
    dp1, dw1, alpha1 = step_of(dir3, small3, tb)
    image = shifted + mm(dw1, pv[...], NN)
    residual = source - alpha1 * image
    margin3 = margin_next - alpha1 * (small3[:, :tb] + mm(dw1, kp, NT))
    search2 = (precond * residual).astype(BF16).astype(F32) - mm(
        margin3.astype(BF16), okall[:tb, :], NN
    )
    x4 = send_direction(search2, dir4)
    sm4[ga, :, 0:1] = jnp.sum(residual * search2, axis=1, keepdims=True)
    sm4[ga, :, 1:2] = jnp.sum(shift * search2 * search2, axis=1, keepdims=True)
    for b, col in enumerate(overlaps(search2)):
        sm4[ga, :, 5 + b : 6 + b] = col
    x4.append(exchange(sm4, "ga").start())

    for x in x4:
        x.wait()
    small4 = total(sm4, nga)
    dp2, _, alpha2 = step_of(dir4, small4, 0)
    resp_proj = alpha1 * dp1 + alpha2 * dp2
    pairs[...] = jnp.zeros_like(pairs)
    for a in range(3):
        left = resp_proj[a * bands : (a + 1) * bands]
        for b in range(3):
            right = proj[(1 + b) * bands : (2 + b) * bands]
            pairs[3 * a + b : 3 * a + b + 1, :] = strength * jnp.sum(
                left * right, axis=0, keepdims=True
            )
    born = mm(pairs[...], onehot.astype(F32), NT, lax.Precision.HIGHEST)
    diel = alpha1 * small4[:, 2:5] + alpha2 * small4[:, 5:8]
    fin[bd, 0:16, :] = born
    fin[bd, 16:24, :] = jnp.zeros((8, born.shape[1]), F32)
    for a in range(3):
        fin[bd, 16 + a : 17 + a, 0:3] = jnp.sum(
            diel[a * bands : (a + 1) * bands], axis=0, keepdims=True
        )
    xf = exchange(fin, "band").start()
    response = alpha1 * search + alpha2 * search2
    for a in range(3):
        resp_ref[a] = response[a * bands : (a + 1) * bands].astype(BF16)
    xf.wait()
    final = total(fin, nband)
    born_ref[...] = BORN_SCALE * final[0:9]
    eye = (
        lax.broadcasted_iota(jnp.int32, (3, 3), 0) == lax.broadcasted_iota(jnp.int32, (3, 3), 1)
    ).astype(F32)
    diel_ref[...] = eye + (4.0 / tb) * final[16:19, 0:3]

    for x in [x0, *x1, xk, xg, x2, xa, *x3, *x4, xf]:
        x.drain()


def solution(mesh):
    nga, nband = mesh.shape["ga"], mesh.shape["band"]

    def per_device(
        orbitals, energies, projectors, miller_index, recip_scale, species, proj_atom, coupling
    ):
        bands, width = orbitals.shape
        nproj = projectors.shape[0]
        natoms = species.shape[0]
        tb = bands * nband
        rows = 3 * bands
        pchunks = 4
        smw = -(-(tb + 8) // 128) * 128
        axes = ["band"] + ["ga"] * pchunks + ["ga", "ga", "ga", "band"]
        axes += (["ga"] * pchunks + ["ga"]) * 2 + ["band"]
        sems = []
        for axis in axes:
            sems += [pltpu.SemaphoreType.DMA((mesh.shape[axis],))] * 2
        vmem = pl.BlockSpec(memory_space=pltpu.VMEM)
        smem = pl.BlockSpec(memory_space=pltpu.SMEM)
        return pl.pallas_call(
            functools.partial(kernel, nga, nband, pchunks),
            out_shape=(
                jax.ShapeDtypeStruct((3, bands, width), BF16),
                jax.ShapeDtypeStruct((3, 3), F32),
                jax.ShapeDtypeStruct((9, natoms), F32),
            ),
            in_specs=[
                vmem,
                smem,
                pl.BlockSpec(memory_space=pl.ANY),
                vmem,
                smem,
                vmem,
                vmem,
                smem,
            ],
            out_specs=(vmem, vmem, vmem),
            scratch_shapes=[
                pltpu.VMEM((nproj, width), BF16),
                pltpu.VMEM((nband, bands, width), BF16),
                pltpu.VMEM((tb, width), F32),
                pltpu.VMEM((2 * tb, width), BF16),
                pltpu.VMEM((nga, 4 * bands, nproj), BF16),
                pltpu.VMEM((nga, bands, nproj), BF16),
                pltpu.VMEM((nband, bands, nproj), BF16),
                pltpu.VMEM((tb, nproj), F32),
                pltpu.VMEM((nga, tb, tb), F32),
                pltpu.VMEM((nga, rows, 2 * tb), F32),
                pltpu.VMEM((nga, rows, nproj), BF16),
                pltpu.VMEM((nga, rows, smw), F32),
                pltpu.VMEM((nga, rows, nproj), BF16),
                pltpu.VMEM((nga, rows, 128), F32),
                pltpu.VMEM((nband, 24, natoms), F32),
                pltpu.VMEM((16, nproj), F32),
                pltpu.SemaphoreType.DMA((pchunks,)),
                *sems,
            ],
            compiler_params=pltpu.CompilerParams(
                collective_id=0, has_side_effects=True, vmem_limit_bytes=48 * 1024 * 1024
            ),
        )(
            orbitals,
            energies,
            projectors,
            miller_index,
            recip_scale,
            species.reshape(1, natoms),
            proj_atom.reshape(1, nproj),
            coupling,
        )

    placed = (
        P(("grp", "band"), "ga"),
        P(("grp", "band")),
        P("grp", "ga"),
        P(None, "ga"),
        P("grp"),
        P(),
        P(),
        P(),
    )
    return jax.shard_map(
        per_device,
        mesh=mesh,
        in_specs=placed,
        out_specs=(P(None, ("grp", "band"), "ga"), P("grp", None), P(None, "grp")),
        check_vma=False,
    )
```

time: 193 us -> 42.2 us (0.22)
  blocking collectives: 125 us -> 0 us
  Pallas kernels: 0 us -> 32.9 us
  waiting for transfers between devices: 29.9 us -> 0 us
  matrix products: 14.5 us -> 0 us
  between operations: 14.2 us -> 0.66 us
  other arithmetic: 4.39 us -> 0 us
  local copies, waits for them, and re-layouts: 3.93 us -> 8.24 us
    psum x7 -> x0, blocking collectives: 119 us -> none  [the longest x3 49.6 us: conduct(): margin = lax.psum(block, 'ga').astype(jnp.bfloat16)]
    pallas_call x0 -> x1, Pallas kernels: none -> 32.9 us  [per_device(): pl.pallas_call(functools.partial(kernel, nga, nband, pchunks), out_shape=...]
    psum x1 -> x0, waiting for transfers between devices: 29.9 us -> none  [per_device(): proj = lax.psum(proj_local, 'ga').reshape(4, bands, nproj)]
    dot_general x16 -> x0, matrix products: 14.5 us -> none  [the longest x1 5.93 us: per_device(): jnp.einsum('anp,bnp->abp', resp_proj, proj[1:], precision=lax.Precision.H...]
    unnamed x14 -> x19, local copies, waits for them, and re-layouts: 0.04 us -> 8.24 us
    all_gather x1 -> x0, blocking collectives: 6.51 us -> none  [conduct(): lax.all_gather(orbitals, 'band', axis=0, tiled=True)]
  transfers between devices with their start and end apart: 1 -> 0, of which waited for: 1 -> 0; matrix products, arithmetic and copies ran while one was open for 0% -> 0% of each run, Pallas kernels for 0% -> 0%
where the time goes in v1:
time: 42.2 us; the launch traced here: 41.8 us
  Pallas kernels  32.9 us (78%)
  local copies, waits for them, and re-layouts  8.24 us (20%)
  between operations  0.66 us (2%)
    pallas_call x1, Pallas kernels, per_device(): pl.pallas_call(functools.partial(kernel, nga, nband, pchunks), out_shape=...  32.9 us
    unnamed x19, local copies, waits for them, and re-layouts  8.24 us

profile of v1, /device:TPU:0, one launch (start us, length us, event | category | flops | bytes accessed | tf_op | source)
XLA Modules:
  0.0 41.8 jit_solution(6789004515470615722)
XLA Ops:
  0.6 0.0 copy-start
  0.6 1.6 %copy-done = bf16[512,2048]{1,0:T(8,128)(2,1)S(1)} copy-done((bf16[512,2048]{1,0:T(8,128)(2,1)S(1)}, bf16[512,2048]{1,0:T(8,128)(2,1)}, u32[]{:S(2)}) %copy-start) | copy-done | bytes 2097176
  2.2 0.0 copy-start.1
  2.2 0.8 %copy-done.1 = bf16[8,2048]{1,0:T(8,128)(2,1)S(1)} copy-done((bf16[8,2048]{1,0:T(8,128)(2,1)S(1)}, bf16[8,2048]{1,0:T(8,128)(2,1)}, u32[]{:S(2)}) %copy-start.1) | copy-done | bytes 32792
  3.0 0.0 copy-start.2
  3.0 0.8 %copy-done.2 = s32[3,2048]{1,0:T(4,128)S(1)} copy-done((s32[3,2048]{1,0:T(4,128)S(1)}, s32[3,2048]{1,0:T(4,128)}, u32[]{:S(2)}) %copy-start.2) | copy-done | bytes 24600
  3.7 0.0 copy-start.3
  3.7 0.7 %copy-done.3 = s32[512]{0:T(512)S(1)} copy-done((s32[512]{0:T(512)S(1)}, s32[512]{0:T(512)}, u32[]{:S(2)}) %copy-start.3) | copy-done | bytes 2072
  4.4 0.0 copy-start.4
  4.4 0.7 %copy-done.4 = f32[3,4]{1,0:T(4,128)S(1)} copy-done((f32[3,4]{1,0:T(4,128)S(1)}, f32[3,4]{1,0:T(4,128)}, u32[]{:S(2)}) %copy-start.4) | copy-done | bytes 72
  5.1 0.0 copy-start.5
  5.1 0.7 %copy-done.5 = f32[8]{0:T(128)S(1)} copy-done((f32[8]{0:T(128)S(1)}, f32[8]{0:T(128)}, u32[]{:S(2)}) %copy-start.5) | copy-done | bytes 56
  5.8 0.0 copy-start.6
  5.8 0.7 %copy-done.6 = f32[3]{0:T(128)S(1)} copy-done((f32[3]{0:T(128)S(1)}, f32[3]{0:T(128)}, u32[]{:S(2)}) %copy-start.6) | copy-done | bytes 36
  6.4 0.0 copy-start.7
  6.4 0.7 %copy-done.7 = s32[128]{0:T(128)S(1)} copy-done((s32[128]{0:T(128)S(1)}, s32[128]{0:T(128)}, u32[]{:S(2)}) %copy-start.7) | copy-done | bytes 536
  7.1 32.9 %shard_map.103 = (bf16[3,8,2048]{2,1,0:T(8,128)(2,1)S(1)}, f32[3,3]{1,0:T(4,128)S(1)}, f32[9,128]{1,0:T(8,128)S(1)}) custom-call(bf16[8,2048]{1,0:T(8,128)(2,1)S(1)} %copy-done.1, f32[8]{0:T(128)S(1)} %copy-done.5, bf16[512,2048]{1,0:T(8,128)(2,1)S(1)} %copy-done, s32[3,2048]{1,0:T(4,128)S(1)} %copy-done.2, f32[3]{0:T(128)S(1)} %copy-done.6, ...), custom_call_target="tpu_custom_call" | custom-call | tf_op jit(solution)/shard_map/pallas_call | solution.py:335
  40.0 0.6 %copy.14 = bf16[3,8,2048]{2,1,0:T(8,128)(2,1)} copy(bf16[3,8,2048]{2,1,0:T(8,128)(2,1)S(1)} %get-tuple-element.6) | data formatting | bytes 196608
  40.7 0.6 %copy.15 = f32[3,3]{1,0:T(4,128)} copy(f32[3,3]{1,0:T(4,128)S(1)} %get-tuple-element.7) | data formatting | bytes 72
  41.2 0.6 %copy.16 = f32[9,128]{1,0:T(8,128)} copy(f32[9,128]{1,0:T(8,128)S(1)} %get-tuple-element.8) | data formatting | bytes 9216
Async XLA Ops:
  0.6 1.6 %copy-start = (bf16[512,2048]{1,0:T(8,128)(2,1)S(1)}, bf16[512,2048]{1,0:T(8,128)(2,1)}, u32[]{:S(2)}) copy-start(bf16[512,2048]{1,0:T(8,128)(2,1)} %proj_hbm.1) | copy-start | bytes 6291460
  2.2 0.8 %copy-start.1 = (bf16[8,2048]{1,0:T(8,128)(2,1)S(1)}, bf16[8,2048]{1,0:T(8,128)(2,1)}, u32[]{:S(2)}) copy-start(bf16[8,2048]{1,0:T(8,128)(2,1)} %orb_ref.1) | copy-start | bytes 98308
  3.0 0.8 %copy-start.2 = (s32[3,2048]{1,0:T(4,128)S(1)}, s32[3,2048]{1,0:T(4,128)}, u32[]{:S(2)}) copy-start(s32[3,2048]{1,0:T(4,128)} %miller_ref.1) | copy-start | bytes 73732
  3.7 0.7 %copy-start.3 = (s32[512]{0:T(512)S(1)}, s32[512]{0:T(512)}, u32[]{:S(2)}) copy-start(s32[512]{0:T(512)} %param.14) | copy-start | bytes 6148
  4.4 0.7 %copy-start.4 = (f32[3,4]{1,0:T(4,128)S(1)}, f32[3,4]{1,0:T(4,128)}, u32[]{:S(2)}) copy-start(f32[3,4]{1,0:T(4,128)} %coupling_ref.1) | copy-start | bytes 148
  5.1 0.7 %copy-start.5 = (f32[8]{0:T(128)S(1)}, f32[8]{0:T(128)}, u32[]{:S(2)}) copy-start(f32[8]{0:T(128)} %energy_ref.1) | copy-start | bytes 100
  5.8 0.7 %copy-start.6 = (f32[3]{0:T(128)S(1)}, f32[3]{0:T(128)}, u32[]{:S(2)}) copy-start(f32[3]{0:T(128)} %recip_ref.1) | copy-start | bytes 40
  6.4 0.7 %copy-start.7 = (s32[128]{0:T(128)S(1)}, s32[128]{0:T(128)}, u32[]{:S(2)}) copy-start(s32[128]{0:T(128)} %param.13) | copy-start | bytes 1540

commit v2 on v1

--- a/solution.py
+++ b/solution.py
@@ -74,17 +74,25 @@
     nga,
     nband,
     pchunks,
+    orb_hbm,
+    energy_hbm,
+    proj_hbm,
+    miller_hbm,
+    recip_hbm,
+    species_hbm,
+    atom_hbm,
+    coupling_hbm,
+    resp_ref,
+    diel_ref,
+    born_ref,
     orb_ref,
     energy_ref,
-    proj_hbm,
     miller_ref,
     recip_ref,
     species_ref,
     atom_ref,
     coupling_ref,
-    resp_ref,
-    diel_ref,
-    born_ref,
+    lsem,
     pv,
     oall,
     ofull,
@@ -94,7 +102,8 @@
     kall,
     kfull,
     gram,
-    r2,
+    gall,
+    gfull,
     dir3,
     sm3,
     dir4,
@@ -121,6 +130,20 @@
         pl.semaphore_signal(
             barrier, inc=1, device_id={"band": lax.rem(bd + off, nband)}, device_id_type=MESH
         )
+    small = []
+    for i, (src, dst) in enumerate(
+        [
+            (orb_hbm, orb_ref),
+            (miller_hbm, miller_ref),
+            (recip_hbm, recip_ref),
+            (energy_hbm, energy_ref),
+            (species_hbm, species_ref),
+            (atom_hbm, atom_ref),
+            (coupling_hbm, coupling_ref),
+        ]
+    ):
+        small.append(pltpu.make_async_copy(src, dst, lsem.at[i]))
+        small[-1].start()
     loads = []
     for k in range(pchunks):
         part = pl.ds(k * pc, pc)
@@ -133,6 +156,8 @@
         n, me = (nga, ga) if axis == "ga" else (nband, bd)
         return Exchange(buf, next(it), next(it), axis, n, me, pick)
 
+    for load in small:
+        load.wait()
     orb = orb_ref[...].astype(F32)
     wave = [miller_ref[d : d + 1, :].astype(F32) * recip_ref[d] for d in range(3)]
     kinetic = 0.5 * (wave[0] * wave[0] + wave[1] * wave[1] + wave[2] * wave[2])
@@ -145,8 +170,8 @@
     ecol = jnp.zeros((bands, 1), F32)
     for n in range(bands):
         ecol = jnp.where(band_row == n, energy_ref[n], ecol)
+    ecol = jnp.concatenate([ecol] * 3, axis=0)
     shift = kinetic - ecol
-    shift = jnp.concatenate([shift] * 3, axis=0)
 
     natoms = species_ref.shape[1]
     atoms = lax.broadcasted_iota(jnp.int32, (natoms, nproj), 0)
@@ -181,10 +206,12 @@
     x0.wait()
     for j in range(nband):
         ofull[j * bands : (j + 1) * bands, :] = oall[j].astype(F32)
-    occupied = ofull[...].astype(BF16)
-    okall[:tb, :] = occupied
-    okall[tb:, :] = (precond * ofull[...]).astype(BF16)
-    gram[ga] = mm(occupied, okall[tb:, :], NT)
+    every = ofull[...]
+    okall[:tb, :] = every.astype(BF16)
+    okall[tb : 2 * tb, :] = (precond * every).astype(BF16)
+    okall[2 * tb : 3 * tb, :] = (precond * precond * every).astype(BF16)
+    okall[3 * tb :, :] = (kinetic * every).astype(BF16)
+    gram[ga] = mm(orb_ref[...], okall[...], NT)
     xg = exchange(gram, "ga").start()
 
     for x in x1:
@@ -196,26 +223,7 @@
     comm = jnp.concatenate(
         [wave[d] * inner + returned[(1 + d) * bands : (2 + d) * bands] for d in range(3)], axis=0
     ).astype(BF16)
-    r2[ga] = mm(comm, okall[...], NT)
-    x2 = exchange(r2, "ga").start()
-
-    xk.wait()
-    kall[bd] = total(kk, nga).astype(BF16)
-    xa = exchange(kall, "band").start()
-
-    xg.wait()
-    gram_all = total(gram, nga)
-    x2.wait()
-    both = total(r2, nga)
-    margin = both[:, :tb].astype(BF16)
-    margin_next = mm(margin.astype(F32), gram_all, NN, lax.Precision.HIGHEST) - both[:, tb:]
-    removed = mm(
-        jnp.concatenate([margin.astype(F32), margin_next], axis=0).astype(BF16),
-        okall[:tb, :],
-        NN,
-    )
-    source = removed[:rows] - comm.astype(F32)
-    search = (precond * source).astype(BF16).astype(F32) - removed[rows:]
+    comm_float = comm.astype(F32)
 
     def send_direction(found, buf):
         low = found.astype(BF16)
@@ -225,6 +233,65 @@
             buf[ga, :, part] = mm(low, pv[part, :], NT).astype(BF16)
             out.append(exchange(buf, "ga", (slice(None), part)).start())
         return out
+
+    scaled = precond * comm_float
+    x3 = send_direction(scaled, dir3)
+    sm3[ga, :, : 3 * tb] = mm(comm, okall[: 3 * tb, :], NT)
+    sm3[ga, :, 3 * tb : 3 * tb + 1] = jnp.sum(scaled * comm_float, axis=1, keepdims=True)
+    sm3[ga, :, 3 * tb + 1 : 3 * tb + 2] = jnp.sum(scaled * scaled, axis=1, keepdims=True)
+    x3.append(exchange(sm3, "ga").start())
+
+    xk.wait()
+    xg.wait()
+    kall[bd, :, :nproj] = proj[:bands].astype(BF16)
+    kall[bd, :, nproj:] = total(kk, nga).astype(BF16)
+    gall[bd] = total(gram, nga)
+    xa = [exchange(kall, "band").start(), exchange(gall, "band").start()]
+    for x in xa:
+        x.wait()
+    for j in range(nband):
+        kfull[j * bands : (j + 1) * bands, :] = kall[j].astype(F32)
+        gfull[j * bands : (j + 1) * bands, :] = gall[j]
+    pp = kfull[:, :nproj].astype(BF16)
+    kp = kfull[:, nproj:].astype(BF16)
+    grams = gfull[...]
+    g1, gk, gk2, gkin = [grams[:, q * tb : (q + 1) * tb] for q in range(4)]
+
+    def hi(a, b):
+        return mm(a, b, NN, lax.Precision.HIGHEST)
+
+    for x in x3:
+        x.wait()
+    small3 = total(sm3, nga)
+    u, v, w = [small3[:, q * tb : (q + 1) * tb] for q in range(3)]
+    ckc = small3[:, 3 * tb : 3 * tb + 1]
+    ck2c = small3[:, 3 * tb + 1 : 3 * tb + 2]
+    margin_low = u.astype(BF16)
+    margin = margin_low.astype(F32)
+    a1k, a2k = hi(margin, gk), hi(margin, gk2)
+    margin_next = a1k - v
+    next_low = margin_next.astype(BF16)
+    nxt = next_low.astype(F32)
+    b1, bk, bkin = hi(nxt, g1), hi(nxt, gk), hi(nxt, gkin)
+    numerator = ckc + jnp.sum(
+        margin * (a1k - 2.0 * v - b1) + nxt * u, axis=1, keepdims=True
+    )
+    diag = (ckc - ck2c - ecol * ck2c) + jnp.sum(
+        margin * (a1k - a2k - 2.0 * (v - w) - 2.0 * (b1 - bk))
+        + nxt * (2.0 * (u - v) + bkin)
+        - ecol * (margin * (a2k - 2.0 * w - 2.0 * bk) + nxt * (2.0 * v + b1)),
+        axis=1,
+        keepdims=True,
+    )
+    margin_step = (a1k - a2k) - (v - w) - (b1 - bk) - ecol * (a2k - w - bk)
+    dp1 = mm(margin_low, kp, NN) - mm(next_low, pp, NN) - total(dir3, nga)
+    dw1 = (strength * dp1).astype(BF16)
+    alpha1 = numerator / (
+        diag + jnp.sum(dw1.astype(F32) * dp1, axis=1, keepdims=True)
+    )
+    removed = mm(jnp.concatenate([margin, nxt], axis=0).astype(BF16), okall[:tb, :], NN)
+    source = removed[:rows] - comm_float
+    search = precond * source - removed[rows:]
 
     def overlaps(found):
         return [
@@ -244,31 +311,16 @@
         )
         return dp, dw, small[:, col : col + 1] / curvature
 
-    x3 = send_direction(search, dir3)
     shifted = shift * search
-    sm3[ga, :, :tb] = mm((precond * shifted).astype(BF16), okall[:tb, :], NT)
-    sm3[ga, :, tb : tb + 1] = jnp.sum(source * search, axis=1, keepdims=True)
-    sm3[ga, :, tb + 1 : tb + 2] = jnp.sum(shifted * search, axis=1, keepdims=True)
-    x3.append(exchange(sm3, "ga").start())
-
+    image = shifted + mm(dw1, pv[...], NN)
+    residual = source - alpha1 * image
+    margin3 = margin_next - alpha1 * (margin_step + mm(dw1, kp, NT))
+    search2 = (precond * residual).astype(BF16).astype(F32) - mm(
+        margin3.astype(BF16), okall[:tb, :], NN
+    )
+    x4 = send_direction(search2, dir4)
     for b, col in enumerate(overlaps(search)):
         sm4[ga, :, 2 + b : 3 + b] = col
-    xa.wait()
-    for j in range(nband):
-        kfull[j * bands : (j + 1) * bands, :] = kall[j].astype(F32)
-    kp = kfull[...].astype(BF16)
-
-    for x in x3:
-        x.wait()
-    small3 = total(sm3, nga)
-    dp1, dw1, alpha1 = step_of(dir3, small3, tb)
-    image = shifted + mm(dw1, pv[...], NN)
-    residual = source - alpha1 * image
-    margin3 = margin_next - alpha1 * (small3[:, :tb] + mm(dw1, kp, NT))
-    search2 = (precond * residual).astype(BF16).astype(F32) - mm(
-        margin3.astype(BF16), okall[:tb, :], NN
-    )
-    x4 = send_direction(search2, dir4)
     sm4[ga, :, 0:1] = jnp.sum(residual * search2, axis=1, keepdims=True)
     sm4[ga, :, 1:2] = jnp.sum(shift * search2 * search2, axis=1, keepdims=True)
     for b, col in enumerate(overlaps(search2)):
@@ -308,7 +360,7 @@
     ).astype(F32)
     diel_ref[...] = eye + (4.0 / tb) * final[16:19, 0:3]
 
-    for x in [x0, *x1, xk, xg, x2, xa, *x3, *x4, xf]:
+    for x in [x0, *x1, xk, xg, *x3, *xa, *x4, xf]:
         x.drain()
 
 
@@ -324,14 +376,13 @@
         tb = bands * nband
         rows = 3 * bands
         pchunks = 4
-        smw = -(-(tb + 8) // 128) * 128
-        axes = ["band"] + ["ga"] * pchunks + ["ga", "ga", "ga", "band"]
-        axes += (["ga"] * pchunks + ["ga"]) * 2 + ["band"]
+        smw = -(-(3 * tb + 8) // 128) * 128
+        axes = ["band"] + ["ga"] * pchunks + ["ga", "ga"]
+        axes += ["ga"] * pchunks + ["ga", "band", "band"] + ["ga"] * pchunks + ["ga", "band"]
         sems = []
         for axis in axes:
             sems += [pltpu.SemaphoreType.DMA((mesh.shape[axis],))] * 2
         vmem = pl.BlockSpec(memory_space=pltpu.VMEM)
-        smem = pl.BlockSpec(memory_space=pltpu.SMEM)
         return pl.pallas_call(
             functools.partial(kernel, nga, nband, pchunks),
             out_shape=(
@@ -339,28 +390,28 @@
                 jax.ShapeDtypeStruct((3, 3), F32),
                 jax.ShapeDtypeStruct((9, natoms), F32),
             ),
-            in_specs=[
-                vmem,
-                smem,
-                pl.BlockSpec(memory_space=pl.ANY),
-                vmem,
-                smem,
-                vmem,
-                vmem,
-                smem,
-            ],
+            in_specs=[pl.BlockSpec(memory_space=pltpu.HBM)] * 8,
             out_specs=(vmem, vmem, vmem),
             scratch_shapes=[
+                pltpu.VMEM(orbitals.shape, BF16),
+                pltpu.SMEM(energies.shape, F32),
+                pltpu.VMEM(miller_index.shape, jnp.int32),
+                pltpu.SMEM(recip_scale.shape, F32),
+                pltpu.VMEM((1, natoms), jnp.int32),
+                pltpu.VMEM((1, nproj), jnp.int32),
+                pltpu.SMEM(coupling.shape, F32),
+                pltpu.SemaphoreType.DMA((7,)),
                 pltpu.VMEM((nproj, width), BF16),
                 pltpu.VMEM((nband, bands, width), BF16),
                 pltpu.VMEM((tb, width), F32),
-                pltpu.VMEM((2 * tb, width), BF16),
+                pltpu.VMEM((4 * tb, width), BF16),
                 pltpu.VMEM((nga, 4 * bands, nproj), BF16),
                 pltpu.VMEM((nga, bands, nproj), BF16),
-                pltpu.VMEM((nband, bands, nproj), BF16),
-                pltpu.VMEM((tb, nproj), F32),
-                pltpu.VMEM((nga, tb, tb), F32),
-                pltpu.VMEM((nga, rows, 2 * tb), F32),
+                pltpu.VMEM((nband, bands, 2 * nproj), BF16),
+                pltpu.VMEM((tb, 2 * nproj), F32),
+                pltpu.VMEM((nga, bands, 4 * tb), F32),
+                pltpu.VMEM((nband, bands, 4 * tb), F32),
+                pltpu.VMEM((tb, 4 * tb), F32),
                 pltpu.VMEM((nga, rows, nproj), BF16),
                 pltpu.VMEM((nga, rows, smw), F32),
                 pltpu.VMEM((nga, rows, nproj), BF16),
@@ -371,7 +422,7 @@
                 *sems,
             ],
             compiler_params=pltpu.CompilerParams(
-                collective_id=0, has_side_effects=True, vmem_limit_bytes=48 * 1024 * 1024
+                collective_id=0, has_side_effects=True, vmem_limit_bytes=67_043_328
             ),
         )(
             orbitals,

time: 42.2 us -> 33.6 us (0.80)
  Pallas kernels: 32.9 us -> 28.6 us
  local copies, waits for them, and re-layouts: 8.24 us -> 4.08 us
    pallas_call x1, Pallas kernels: 32.9 us -> 28.6 us  [per_device(): pl.pallas_call(functools.partial(kernel, nga, nband, pchunks), out_shape=...]
    unnamed x19 -> x3, local copies, waits for them, and re-layouts: 8.24 us -> 4.08 us
where the time goes in v2:
time: 33.6 us; the launch traced here: 33.4 us
  Pallas kernels  28.6 us (85%)
  local copies, waits for them, and re-layouts  4.08 us (12%)
  between operations  0.64 us (2%)
    pallas_call x1, Pallas kernels, per_device(): pl.pallas_call(functools.partial(kernel, nga, nband, pchunks), out_shape=...  28.6 us
    unnamed x3, local copies, waits for them, and re-layouts  4.08 us

profile of v2, /device:TPU:0, one launch (start us, length us, event | category | flops | bytes accessed | tf_op | source)
XLA Modules:
  0.0 33.4 jit_solution(17758445201504161812)
XLA Ops:
  0.6 28.6 %shard_map.103 = (bf16[3,8,2048]{2,1,0:T(8,128)(2,1)}, f32[3,3]{1,0:T(4,128)}, f32[9,128]{1,0:T(8,128)}) custom-call(bf16[8,2048]{1,0:T(8,128)(2,1)} %orb_hbm.1, f32[8]{0:T(128)} %energy_hbm.1, bf16[512,2048]{1,0:T(8,128)(2,1)} %proj_hbm.1, s32[3,2048]{1,0:T(4,128)} %miller_hbm.1, f32[3]{0:T(128)} %recip_hbm.1, s32[1,128]{1,0:T(1,128)} %bitcast.3, ...), custom_call_target="tpu_custom_call" | custom-call | tf_op jit(solution)/shard_map/pallas_call | solution.py:386
  29.3 1.5 %copy.14 = bf16[3,8,2048]{2,1,0:T(8,128)(2,1)} copy(bf16[3,8,2048]{2,1,0:T(8,128)(2,1)} %get-tuple-element.6) | data formatting | bytes 196608
  30.8 1.2 %copy.15 = f32[3,3]{1,0:T(4,128)} copy(f32[3,3]{1,0:T(4,128)} %get-tuple-element.7) | data formatting | bytes 72
  32.1 1.3 %copy.16 = f32[9,128]{1,0:T(8,128)} copy(f32[9,128]{1,0:T(8,128)} %get-tuple-element.8) | data formatting | bytes 9216

commit v3 on v2

--- a/solution.py
+++ b/solution.py
@@ -166,6 +166,21 @@
         [orb] + [wave[d] * orb for d in range(3)] + [precond * orb], axis=0
     ).astype(BF16)
 
+    pl.semaphore_wait(barrier, nga + nband - 2)
+
+    oall[bd] = orb_ref[...]
+    x0 = exchange(oall, "band").start()
+
+    x1 = []
+    for k in range(pchunks):
+        loads[k].wait()
+        part = pl.ds(k * pc, pc)
+        piece = mm(stacked, pv[part, :], NT)
+        r1[ga, :, part] = piece[: 4 * bands].astype(BF16)
+        kk[ga, :, part] = piece[4 * bands :].astype(BF16)
+        x1.append(exchange(r1, "ga", (slice(None), part)).start())
+    xk = exchange(kk, "ga").start()
+
     band_row = lax.broadcasted_iota(jnp.int32, (bands, 1), 0)
     ecol = jnp.zeros((bands, 1), F32)
     for n in range(bands):
@@ -187,21 +202,6 @@
             strength = jnp.where(
                 jnp.logical_and(spec == float(s), chan == c), coupling_ref[s, c], strength
             )
-
-    pl.semaphore_wait(barrier, nga + nband - 2)
-
-    oall[bd] = orb_ref[...]
-    x0 = exchange(oall, "band").start()
-
-    x1 = []
-    for k in range(pchunks):
-        loads[k].wait()
-        part = pl.ds(k * pc, pc)
-        piece = mm(stacked, pv[part, :], NT)
-        r1[ga, :, part] = piece[: 4 * bands].astype(BF16)
-        kk[ga, :, part] = piece[4 * bands :].astype(BF16)
-        x1.append(exchange(r1, "ga", (slice(None), part)).start())
-    xk = exchange(kk, "ga").start()
 
     x0.wait()
     for j in range(nband):
@@ -364,6 +364,18 @@
         x.drain()
 
 
+def finish(resp, diel, born, resp_out, diel_out, born_out, sem):
+    copies = [
+        pltpu.make_async_copy(resp, resp_out, sem.at[0]),
+        pltpu.make_async_copy(diel, diel_out, sem.at[1]),
+        pltpu.make_async_copy(born, born_out, sem.at[2]),
+    ]
+    for copy in copies:
+        copy.start()
+    for copy in copies:
+        copy.wait()
+
+
 def solution(mesh):
     nga, nband = mesh.shape["ga"], mesh.shape["band"]
 
@@ -375,7 +387,7 @@
         natoms = species.shape[0]
         tb = bands * nband
         rows = 3 * bands
-        pchunks = 4
+        pchunks = 2
         smw = -(-(3 * tb + 8) // 128) * 128
         axes = ["band"] + ["ga"] * pchunks + ["ga", "ga"]
         axes += ["ga"] * pchunks + ["ga", "band", "band"] + ["ga"] * pchunks + ["ga", "band"]
@@ -383,12 +395,12 @@
         for axis in axes:
             sems += [pltpu.SemaphoreType.DMA((mesh.shape[axis],))] * 2
         vmem = pl.BlockSpec(memory_space=pltpu.VMEM)
-        return pl.pallas_call(
+        parts = pl.pallas_call(
             functools.partial(kernel, nga, nband, pchunks),
             out_shape=(
-                jax.ShapeDtypeStruct((3, bands, width), BF16),
-                jax.ShapeDtypeStruct((3, 3), F32),
-                jax.ShapeDtypeStruct((9, natoms), F32),
+                pltpu.VMEM((3, bands, width), BF16),
+                pltpu.VMEM((3, 3), F32),
+                pltpu.VMEM((9, natoms), F32),
             ),
             in_specs=[pl.BlockSpec(memory_space=pltpu.HBM)] * 8,
             out_specs=(vmem, vmem, vmem),
@@ -422,7 +434,7 @@
                 *sems,
             ],
             compiler_params=pltpu.CompilerParams(
-                collective_id=0, has_side_effects=True, vmem_limit_bytes=67_043_328
+                collective_id=0, has_side_effects=True, vmem_limit_bytes=67_108_864 - 256 * 1024
             ),
         )(
             orbitals,
@@ -434,6 +446,14 @@
             proj_atom.reshape(1, nproj),
             coupling,
         )
+        return pl.pallas_call(
+            finish,
+            out_shape=tuple(jax.ShapeDtypeStruct(x.shape, x.dtype) for x in parts),
+            in_specs=[vmem] * 3,
+            out_specs=[pl.BlockSpec(memory_space=pltpu.HBM)] * 3,
+            scratch_shapes=[pltpu.SemaphoreType.DMA((3,))],
+            compiler_params=pltpu.CompilerParams(vmem_limit_bytes=1024 * 1024),
+        )(*parts)
 
     placed = (
         P(("grp", "band"), "ga"),

time: 33.6 us -> 28.8 us (0.86)
  local copies, waits for them, and re-layouts: 4.08 us -> 0 us
  Pallas kernels: 28.6 us -> 28 us
    unnamed x3 -> x0, local copies, waits for them, and re-layouts: 4.08 us -> none
    pallas_call x1, Pallas kernels: 28.6 us -> 27.3 us  [per_device(): pl.pallas_call(functools.partial(kernel, nga, nband, pchunks), out_shape=...]
    pallas_call x0 -> x1, Pallas kernels: none -> 0.67 us  [per_device(): pl.pallas_call(finish, out_shape=tuple((jax.ShapeDtypeStruct(x.shape, x.d...]
where the time goes in v3:
time: 28.8 us; the launch traced here: 28.6 us
  Pallas kernels  28 us (97%)
  between operations  0.64 us (2%)
    pallas_call x1, Pallas kernels, per_device(): pl.pallas_call(functools.partial(kernel, nga, nband, pchunks), out_shape=...  27.3 us
    pallas_call x1, Pallas kernels, per_device(): pl.pallas_call(finish, out_shape=tuple((jax.ShapeDtypeStruct(x.shape, x.d...  0.67 us

profile of v3, /device:TPU:0, one launch (start us, length us, event | category | flops | bytes accessed | tf_op | source)
XLA Modules:
  0.0 28.6 jit_solution(10706538862642979020)
XLA Ops:
  0.6 27.3 %shard_map.103 = (bf16[3,8,2048]{2,1,0:T(8,128)(2,1)S(1)}, f32[3,3]{1,0:T(4,128)S(1)}, f32[9,128]{1,0:T(8,128)S(1)}) custom-call(bf16[8,2048]{1,0:T(8,128)(2,1)} %orb_hbm.1, f32[8]{0:T(128)} %energy_hbm.1, bf16[512,2048]{1,0:T(8,128)(2,1)} %proj_hbm.1, s32[3,2048]{1,0:T(4,128)} %miller_hbm.1, f32[3]{0:T(128)} %recip_hbm.1, s32[1,128]{1,0:T(1,128)} %bitcast.3, ...), custom_call_target="tpu_custom_call" | custom-call | tf_op jit(solution)/shard_map/pallas_call | solution.py:398
  28.0 0.7 %shard_map.104 = (bf16[3,8,2048]{2,1,0:T(8,128)(2,1)}, f32[3,3]{1,0:T(4,128)}, f32[9,128]{1,0:T(8,128)}) custom-call(bf16[3,8,2048]{2,1,0:T(8,128)(2,1)S(1)} %get-tuple-element.6.resp, f32[3,3]{1,0:T(4,128)S(1)} %get-tuple-element.7.diel, f32[9,128]{1,0:T(8,128)S(1)} %get-tuple-element.8.born), custom_call_target="tpu_custom_call" | custom-call | tf_op jit(solution)/shard_map/pallas_call | solution.py:449
